TPU v7x, 32 devices: a whole 2x2x4 slice. The times are simulated.
32 devices in a mesh: seq: 8 (over z, y), batch: 4 (over x, core).
Axes of the slice: x: 2, y: 2, z: 4, core: 2. Of those that a mesh axis runs over, the one named last changes fastest.
Arguments:
- q_nope: bfloat16 [4, 64, 128, 128], P('batch', None, 'seq'), may hold values from -6 to 6
- q_rope: bfloat16 [4, 64, 128, 64], P('batch', None, 'seq'), may hold values from -8 to 8
- absorb_k: bfloat16 [128, 128, 512], P('seq'), may hold values from -0.5 to 0.5
- absorb_v: bfloat16 [128, 512, 128], P('seq'), may hold values from -0.25 to 0.25
- cache_latent: bfloat16 [4, 8192, 512], P('batch', 'seq'), may hold values from -6 to 6
- cache_rope: bfloat16 [4, 8192, 64], P('batch', 'seq'), may hold values from -8 to 8
- draft_latent: bfloat16 [4, 64, 512], P('batch'), may hold values from -6 to 6
- draft_rope: bfloat16 [4, 64, 64], P('batch'), may hold values from -6 to 6
- residual: bfloat16 [256, 7168], P('batch', 'seq'), may hold values from -1.2 to 1.2
- out_proj: bfloat16 [16384, 7168], P('seq'), may hold values from -0.046875 to 0.046875
- norm_gain: float32 [7168], replicated, may hold values from 0.5 to 1.5
- lm_head: bfloat16 [65536, 7168], P(('seq', 'batch')), may hold values from -2.4095235 to 2.4095235
- parent: int32 [4, 64], replicated, may hold values from 0 to 62, as said below
- draft_ids: int32 [4, 64], replicated, may hold values from 0 to 65535
- cache_len: int32 [4], P('batch'), may hold values from 2048 to 8192
- accept_len: int32 [4], P('batch'), may hold values from 1 to 64
Outputs:
- hidden_out: bfloat16 [256, 7168], P('batch', 'seq')
- target_logp: float32 [4, 64], P('batch')
- accepted_score: float32 [4], P('batch')
Inputs may be any that keep to these rules, and one draw needn't show every extreme that they name: parent[b, 0] = 0, and 0 <= parent[b, i] < i for i >= 1.
All inputs are finite; a program needn't handle non-finite values.
Results may differ from a plain program's by a relative error of at most 0.0095.
Values may be sent and summed in bfloat16 or wider, within the bound.
No kernel may reach another device: no remote copies, remote signals or barrier semaphores. Data moves between devices by JAX's collectives and lax.ppermute only.
A program may use at most 256 MiB of HBM per device.

v0:
```python
import math
import jax
import jax.numpy as jnp
from jax import lax
from jax.sharding import PartitionSpec as P

masked_value = -1e30
norm_epsilon = 1e-06
highest = lax.Precision.HIGHEST


def ancestry_of(parents):
    draft_count = parents.shape[1]
    indices = jnp.arange(draft_count, dtype=jnp.int32)
    parent_map = (
        (parents[:, :, None] == indices[None, None, :]) & (indices[None, :, None] > 0)
    ).astype(jnp.float32)
    ancestry = jnp.broadcast_to(jnp.eye(draft_count, dtype=jnp.float32), parent_map.shape)
    for doubling in range(draft_count.bit_length() - 1):
        ancestry = ancestry + jnp.einsum("rij,rjk->rik", ancestry, parent_map, precision=highest)
        parent_map = jnp.einsum("rij,rjk->rik", parent_map, parent_map, precision=highest)
    return ancestry > 0.5


def body(
    q_nope,
    q_rope,
    absorb_k,
    absorb_v,
    cache_latent,
    cache_rope,
    draft_latent,
    draft_rope,
    residual,
    out_proj,
    norm_gain,
    lm_head,
    parent,
    draft_ids,
    cache_len,
    accept_len,
):
    requests, draft_count, local_heads, nope_width = q_nope.shape
    cache_rows = cache_latent.shape[1]
    score_scale = 1.0 / math.sqrt(nope_width + q_rope.shape[3])
    seq_index = lax.axis_index("seq")
    batch_index = lax.axis_index("batch")
    query_latent = jnp.einsum(
        "rihn,hnc->rihc", q_nope, absorb_k, preferred_element_type=jnp.float32
    ).astype(jnp.bfloat16)
    query_all, rope_all = (
        lax.all_gather(query_latent, "seq", axis=2, tiled=True),
        lax.all_gather(q_rope, "seq", axis=2, tiled=True),
    )
    cache_scores = jnp.einsum(
        "rihc,rtc->rhit", query_all, cache_latent, preferred_element_type=jnp.float32
    )
    cache_scores = cache_scores + jnp.einsum(
        "rihe,rte->rhit", rope_all, cache_rope, preferred_element_type=jnp.float32
    )
    positions = seq_index * cache_rows + jnp.arange(cache_rows, dtype=jnp.int32)
    in_cache = positions[None, :] < cache_len[:, None]
    cache_scores = jnp.where(in_cache[:, None, None, :], cache_scores * score_scale, masked_value)
    tree_scores = jnp.einsum(
        "rihc,rjc->rhij", query_all, draft_latent, preferred_element_type=jnp.float32
    )
    tree_scores = tree_scores + jnp.einsum(
        "rihe,rje->rhij", rope_all, draft_rope, preferred_element_type=jnp.float32
    )
    own_parents = lax.dynamic_slice_in_dim(parent, batch_index * requests, requests, 0)
    ancestry = ancestry_of(own_parents)
    tree_scores = jnp.where(ancestry[:, None, :, :], tree_scores * score_scale, masked_value)
    local_top = jnp.maximum(jnp.max(cache_scores, axis=3), jnp.max(tree_scores, axis=3))
    row_top = lax.pmax(local_top, "seq")
    cache_weights = jnp.exp(cache_scores - row_top[..., None])
    weight_sum = jnp.sum(cache_weights, axis=3)
    partial_value = jnp.einsum(
        "rhit,rtc->rhic",
        cache_weights.astype(jnp.bfloat16),
        cache_latent,
        preferred_element_type=jnp.float32,
    )
    head_first = seq_index * local_heads
    tree_mine = lax.dynamic_slice_in_dim(tree_scores, head_first, local_heads, 1)
    top_mine = lax.dynamic_slice_in_dim(row_top, head_first, local_heads, 1)
    tree_weights = jnp.exp(tree_mine - top_mine[..., None])
    tree_out = jnp.einsum(
        "rhij,rjc->rhic",
        tree_weights.astype(jnp.bfloat16),
        draft_latent,
        preferred_element_type=jnp.float32,
    )
    projected = jnp.einsum(
        "rhic,hcn->rhin",
        partial_value,
        lax.all_gather(absorb_v, "seq", axis=0, tiled=True),
        preferred_element_type=jnp.float32,
    )
    summed, weight_total = (
        lax.psum_scatter(projected, "seq", scatter_dimension=1, tiled=True),
        lax.psum_scatter(weight_sum, "seq", scatter_dimension=1, tiled=True),
    )
    summed = summed + jnp.einsum(
        "rhic,hcn->rhin", tree_out, absorb_v, preferred_element_type=jnp.float32
    )
    weight_total = weight_total + jnp.sum(tree_weights, axis=3)
    head_out = (summed / weight_total[..., None]).astype(jnp.bfloat16)
    head_rows = jnp.transpose(head_out, (0, 2, 1, 3)).reshape(
        requests * draft_count, local_heads * head_out.shape[3]
    )
    branch_term = jnp.dot(head_rows, out_proj, preferred_element_type=jnp.float32)
    width_local = residual.shape[1]
    feature_first = seq_index * width_local
    stream_mine = residual.astype(jnp.float32) + lax.psum_scatter(
        branch_term, "seq", scatter_dimension=1, tiled=True
    )
    square = lax.psum(jnp.sum(stream_mine * stream_mine, axis=1), "seq")
    width_all = width_local * lax.axis_size("seq")
    gain_mine = lax.dynamic_slice_in_dim(norm_gain, feature_first, width_local, 0)
    normed_mine = (
        stream_mine * lax.rsqrt(square / width_all + norm_epsilon)[:, None] * gain_mine
    ).astype(jnp.bfloat16)
    normed = lax.all_gather(normed_mine, "seq", axis=1, tiled=True)
    hidden_out = stream_mine.astype(jnp.bfloat16)
    vocab_rows = lm_head.shape[0]
    vocab_first = lax.axis_index(("seq", "batch")) * vocab_rows
    logits = jnp.einsum(
        "rd,vd->rv",
        lax.all_gather(normed, "batch", axis=0, tiled=True),
        lm_head,
        preferred_element_type=jnp.float32,
    )
    request_total = parent.shape[0]
    parent_rows = (
        jnp.arange(request_total, dtype=jnp.int32)[:, None] * draft_count + parent
    ).reshape(-1)
    source = logits[parent_rows]
    column = jnp.arange(vocab_rows, dtype=jnp.int32) + vocab_first
    picked = jnp.sum(
        jnp.where(column[None, :] == draft_ids.reshape(-1)[:, None], source, 0.0), axis=1
    )
    local_best = jnp.max(logits, axis=1)
    best = lax.pmax(local_best, ("seq", "batch"))
    exp_mass, chosen = lax.psum(
        (jnp.sum(jnp.exp(logits - best[:, None]), axis=1), picked), ("seq", "batch")
    )
    log_total = best + jnp.log(exp_mass)
    target_all = (chosen - log_total[parent_rows]).reshape(request_total, draft_count)
    target_logp = lax.dynamic_slice_in_dim(target_all, batch_index * requests, requests, 0)
    accepted_score = jnp.sum(
        jnp.where(
            jnp.arange(draft_count, dtype=jnp.int32)[None, :] < accept_len[:, None],
            target_logp,
            0.0,
        ),
        axis=1,
    )
    return (hidden_out, target_logp, accepted_score)


def solution(mesh):
    in_specs = (
        P("batch", None, "seq", None),
        P("batch", None, "seq", None),
        P("seq", None, None),
        P("seq", None, None),
        P("batch", "seq", None),
        P("batch", "seq", None),
        P("batch", None, None),
        P("batch", None, None),
        P("batch", "seq"),
        P("seq", None),
        P(),
        P(("seq", "batch"), None),
        P(),
        P(),
        P("batch"),
        P("batch"),
    )
    out_specs = (P("batch", "seq"), P("batch", None), P("batch"))
    return jax.shard_map(body, mesh=mesh, in_specs=in_specs, out_specs=out_specs, check_vma=False)
```

profile of v0, /device:TPU:0, one launch (start us, length us, event | category | flops | bytes accessed | tf_op | source)
XLA Modules:
  0.0 851.1 jit_solution(5020924196684965757)
XLA Ops:
  7.2 1.9 copy.79
  9.1 0.0 all-gather.5.cloned.1.call-start
  9.2 2.4 fusion.25
  11.6 0.0 all-gather.9.cloned.1.call-start
  11.7 0.7 all-gather.9.cloned.1.call-update
  12.3 0.0 reduce-scatter.6.cloned.1.call-start
  12.4 0.2 fusion.68
  12.6 0.2 convolution_add_fusion.5
  12.9 0.2 fusion.81
  13.0 0.2 convolution_add_fusion.4
  13.2 0.2 fusion.82
  13.4 0.2 convolution_add_fusion.3
  13.5 0.2 fusion.83
  13.7 0.2 convolution_add_fusion.2
  13.9 0.2 fusion.84
  14.0 0.2 convolution_add_fusion.1
  14.2 0.2 fusion.41
  14.4 0.1 copy.82
  15.2 46.8 %all-gather.7.cloned.1.call-done = bf16[1,64,128,64]{3,1,0,2:T(8,128)(2,1)} async-done(((bf16[1,64,16,64]{3,1,0,2:T(8,128)(2,1)}), bf16[1,64,128,64]{3,1,0,2:T(8,128)(2,1)}) %all-gather.7.cloned.1.call-update) | async-done | bytes 1048592 | tf_op jit(solution)/shard_map/all_gather | solution.py:53
  62.0 3.5 copy.80
  65.5 4.1 fusion.20
  69.6 13.3 %fusion.42 = f32[1024,64,128]{0,2,1:T(8,128)} fusion(bf16[1,64,128,64]{2,3,1,0:T(8,128)(2,1)S(1)} %copy.80, bf16[1,1024,64]{1,2,0:T(8,128)(2,1)S(1)} %copy-done.7), kind=kOutput, calls=%fused_computation.42 | convolution fusion | flops 1073741824 | bytes 34734080 | tf_op jit(solution)/shard_map/rihe,rte->rhit/dot_general | solution.py:58
  82.9 104.3 %all-gather.5.cloned.1.call-done = bf16[1,64,128,512]{3,1,0,2:T(8,128)(2,1)} async-done(((bf16[1,64,16,512]{3,1,0,2:T(8,128)(2,1)}), bf16[1,64,128,512]{3,1,0,2:T(8,128)(2,1)}) %all-gather.5.cloned.1.call-update) | async-done | bytes 8388624 | tf_op jit(solution)/shard_map/all_gather | solution.py:52
  187.1 10.7 %fusion.79 = (f32[128,64]{1,0:T(8,128)S(1)}, f32[1,128,64,64]{2,3,1,0:T(8,128)}) fusion(f32[64,64,128]{1,0,2:T(8,128)} %fusion.20, bf16[1,64,512]{2,1,0:T(8,128)(2,1)S(1)} %copy-done.8, bf16[1,64,128,512]{3,1,0,2:T(8,128)(2,1)} %all-gather.5.cloned.1.call-done, pred[64,64]{0,1:T(8,128)(4,1)S(1)} %copy.82), kind=kOutput, calls=%fused_computation.93 | convolution fusion | flops 538959872 | bytes 12685312 | tf_op jit(solution)/shard_map/rihc,rjc->rhij/dot_general | solution.py:64
  197.8 0.1 copy.85
  197.9 32.5 %bitcast_reduce_fusion = (f32[128,64]{0,1:T(8,128)S(1)}, f32[1,1024,64,128]{1,3,2,0:T(8,128)}) fusion(f32[1024,64,128]{0,2,1:T(8,128)} %fusion.42, bf16[1,1024,512]{2,1,0:T(8,128)(2,1)S(1)} %copy-done.5, bf16[1,64,128,512]{3,1,0,2:T(8,128)(2,1)} %all-gather.5.cloned.1.call-done, pred[1024]{0:T(1024)(128)(4,1)S(1)} %add_compare_fusion), kind=kOutput, calls=%fused_computation.3 | convolution fusion | flops 8623480832 | bytes 76579840 | tf_op jit(solution)/shard_map/rihc,rtc->rhit/dot_general | solution.py:55
  230.4 37.2 %pmax.14 = f32[1,128,64]{1,2,0:T(8,128)S(1)} all-reduce(f32[1,128,64]{1,2,0:T(8,128)S(1)} %maximum_bitcast_fusion), channel_id=1, replica_groups=mesh['seq'=8,'batch'=4] {'seq'}, use_global_device_ids=true, to_apply=%region_2.3 | all-reduce | flops 8192 | bytes 65536 | tf_op jit(solution)/shard_map/pmax | solution.py:74
  267.6 19.6 %fusion.2 = (f32[128,64]{0,1:T(8,128)S(1)}, bf16[128,64,1024]{2,0,1:T(8,128)(2,1)}) fusion(f32[1,1024,64,128]{1,3,2,0:T(8,128)} %get-tuple-element.12, f32[128,64]{0,1:T(8,128)S(1)} %bitcast.160), kind=kLoop, calls=%fused_computation.8 | loop fusion | flops 25157632 | bytes 50397184 | tf_op jit(solution)/shard_map/reduce_sum | solution.py:76
  287.2 0.7 copy.89
  287.9 0.0 reduce-scatter.4.cloned.1.call-start
  288.0 127.4 %all-gather.9.cloned.1.call-done = bf16[128,512,128]{2,1,0:T(8,128)(2,1)} async-done(((bf16[16,512,128]{2,1,0:T(8,128)(2,1)}), bf16[128,512,128]{2,1,0:T(8,128)(2,1)}) %all-gather.9.cloned.1.call-update) | async-done | bytes 16777232 | tf_op jit(solution)/shard_map/all_gather | solution.py:96
  415.4 27.1 %fusion.17 = f32[1,128,64,128]{3,2,1,0:T(8,128)} fusion(bf16[128,512,128]{2,1,0:T(8,128)(2,1)} %all-gather.9.cloned.1.call-done, bf16[128,64,1024]{2,0,1:T(8,128)(2,1)} %get-tuple-element.8, bf16[1,1024,512]{2,1,0:T(8,128)(2,1)S(1)} %copy-done.5), kind=kOutput, calls=%fused_computation.21 | convolution fusion | flops 9663676416 | bytes 38797312 | tf_op jit(solution)/shard_map/rhic,hcn->rhin/dot_general | solution.py:93
  442.5 0.0 reduce-scatter.8.cloned.1.call-start
  442.6 0.1 constant_dynamic-slice_fusion.1
  442.6 0.1 copy.87
  442.7 1.3 fusion.47
  444.0 0.1 copy.100
  444.1 35.8 %reduce-scatter.6.cloned.1.call-done = f32[1,16,64]{2,0,1:T(1,128)} async-done(((f32[1,128,64]{2,0,1:T(1,128)}), f32[1,16,64]{2,0,1:T(1,128)}) %reduce-scatter.6.cloned.1.call-update) | async-done | bytes 4112 | tf_op jit(solution)/shard_map/reduce_scatter | solution.py:101
  479.9 0.8 copy.91
  480.6 0.1 copy.92
  480.7 90.0 %reduce-scatter.4.cloned.1.call-done = f32[1,16,64,128]{3,2,1,0:T(8,128)} async-done(((f32[1,128,64,128]{3,2,1,0:T(8,128)}), f32[1,16,64,128]{3,2,1,0:T(8,128)}) %reduce-scatter.4.cloned.1.call-update) | async-done | bytes 524304 | tf_op jit(solution)/shard_map/reduce_scatter | solution.py:100
  570.7 2.0 fusion.38
  572.7 0.2 copy.93
  572.9 13.5 %fusion.52 = f32[64,7168]{1,0:T(8,128)} fusion(bf16[2048,7168]{1,0:T(8,128)(2,1)} %param.25, bf16[8,8,16,128]{3,2,1,0:T(8,128)(2,1)S(1)} %bitcast.159), kind=kOutput, calls=%fused_computation.50 | convolution fusion | flops 1879048192 | bytes 31457280 | tf_op jit(solution)/shard_map/dot_general | solution.py:111
  586.4 0.0 all-gather.11.cloned.1.call-start
  586.5 0.8 dynamic_slice.18
  587.3 65.9 %reduce-scatter.8.cloned.1.call-done = f32[64,896]{1,0:T(8,128)} async-done(((f32[64,7168]{1,0:T(8,128)}), f32[64,896]{1,0:T(8,128)}) %reduce-scatter.8.cloned.1.call-update) | async-done | bytes 229392 | tf_op jit(solution)/shard_map/reduce_scatter | solution.py:114
  653.2 1.1 multiply_reduce_fusion
  654.2 19.4 %psum.21 = f32[64]{0:T(128)S(1)} all-reduce(f32[64]{0:T(128)S(1)} %multiply_reduce_fusion), channel_id=1, replica_groups=mesh['seq'=8,'batch'=4] {'seq'}, use_global_device_ids=true, to_apply=%region_9.10 | all-reduce | flops 64 | bytes 512 | tf_op jit(solution)/shard_map/psum | solution.py:117
  673.6 1.6 multiply_convert_fusion
  675.2 35.3 %all_gather.18 = bf16[64,7168]{1,0:T(8,128)(2,1)} all-gather(bf16[64,896]{1,0:T(8,128)(2,1)S(1)} %get-tuple-element.9), channel_id=1, replica_groups=mesh['seq'=8,'batch'=4] {'seq'}, dimensions={1}, use_global_device_ids=true | all-gather | bytes 1032192 | tf_op jit(solution)/shard_map/all_gather | solution.py:123
  710.6 0.1 broadcast_add_fusion
  710.6 0.1 reshape.346
  710.7 0.1 eq.74
  711.5 27.6 %all-gather.11.cloned.1.call-done = bf16[256,7168]{1,0:T(8,128)(2,1)} async-done(((bf16[64,7168]{1,0:T(8,128)(2,1)}), bf16[256,7168]{1,0:T(8,128)(2,1)}) %all-gather.11.cloned.1.call-update) | async-done | bytes 3670032 | tf_op jit(solution)/shard_map/all_gather | solution.py:129
  739.1 14.0 %fusion.80 = (f32[256]{0:T(256)S(1)}, f32[256,2048]{1,0:T(8,128)S(1)}) fusion(bf16[256,7168]{1,0:T(8,128)(2,1)} %all-gather.11.cloned.1.call-done, bf16[2048,7168]{1,0:T(8,128)(2,1)} %param.27), kind=kOutput, calls=%fused_computation.94 | convolution fusion | flops 7516717056 | bytes 35128320 | tf_op jit(solution)/shard_map/rd,vd->rv/dot_general | solution.py:127
  753.1 39.3 %pmax.15 = f32[256]{0:T(256)S(1)} all-reduce(f32[256]{0:T(256)S(1)} %get-tuple-element.15), channel_id=1, replica_groups=mesh['seq'=8,'batch'=4] {'seq','batch'}, use_global_device_ids=true, to_apply=%region_13.14 | all-reduce | flops 256 | bytes 2048 | tf_op jit(solution)/shard_map/pmax | solution.py:143
  792.4 0.4 exponential_reduce_fusion
  792.8 5.3 gather_fusion
  798.2 1.9 select_reduce_fusion
  800.1 41.0 %all-reduce = (f32[256]{0:T(256)S(1)}, f32[256]{0:T(256)S(1)}) all-reduce(f32[256]{0:T(256)S(1)} %select_reduce_fusion, f32[256]{0:T(256)S(1)} %exponential_reduce_fusion), channel_id=1, replica_groups=mesh['seq'=8,'batch'=4] {'seq','batch'}, use_global_device_ids=true, to_apply=%region_11.12 | all-reduce | flops 512 | bytes 4096 | tf_op jit(solution)/shard_map/psum | solution.py:144
  841.1 1.9 gather_fusion.1
  843.0 0.1 reshape.347
  843.1 1.1 fusion.78
  (43 shorter events, 0.3 us)
Async XLA Ops:
  7.2 2.0 copy-start
  7.2 5.2 copy-start.11
  7.2 54.8 %all-gather.7.cloned.1.call-start = ((), (), s32[]{:S(2)}) async-start(), calls=%async_computation.4 | async-start | bytes 2359296 | tf_op jit(solution)/shard_map/all_gather | solution.py:53
  9.1 178.0 %all-gather.5.cloned.1.call-start = ((), (), s32[]{:S(2)}) async-start(), calls=%async_computation.3 | async-start | bytes 9437184 | tf_op jit(solution)/shard_map/all_gather | solution.py:52
  11.6 53.9 %copy-start.9 = (bf16[1,64,64]{2,1,0:T(8,128)(2,1)S(1)}, bf16[1,64,64]{2,1,0:T(8,128)(2,1)}, u32[]{:S(2)}) copy-start(bf16[1,64,64]{2,1,0:T(8,128)(2,1)} %param.23) | copy-start | bytes 24580
  11.6 403.8 %all-gather.9.cloned.1.call-start = ((), (), s32[]{:S(2)}) async-start(), calls=%async_computation.5 | async-start | bytes 18874368 | tf_op jit(solution)/shard_map/all_gather | solution.py:96
  12.3 467.5 %reduce-scatter.6.cloned.1.call-start = ((), (), s32[]{:S(2)}) async-start(), calls=%async_computation.7 | async-start | bytes 73728 | tf_op jit(solution)/shard_map/reduce_scatter | solution.py:101
  15.2 54.4 %copy-start.7 = (bf16[1,1024,64]{1,2,0:T(8,128)(2,1)S(1)}, bf16[1,1024,64]{1,2,0:T(8,128)(2,1)}, u32[]{:S(2)}) copy-start(bf16[1,1024,64]{1,2,0:T(8,128)(2,1)} %param.21) | copy-start | bytes 393220
  62.0 3.5 copy-start.3
  69.6 117.6 %copy-start.8 = (bf16[1,64,512]{2,1,0:T(8,128)(2,1)S(1)}, bf16[1,64,512]{2,1,0:T(8,128)(2,1)}, u32[]{:S(2)}) copy-start(bf16[1,64,512]{2,1,0:T(8,128)(2,1)} %param.22) | copy-start | bytes 196612
  82.9 115.0 %copy-start.5 = (bf16[1,1024,512]{2,1,0:T(8,128)(2,1)S(1)}, bf16[1,1024,512]{2,1,0:T(8,128)(2,1)}, u32[]{:S(2)}) copy-start(bf16[1,1024,512]{2,1,0:T(8,128)(2,1)} %param.20) | copy-start | bytes 3145732
  287.9 282.8 %reduce-scatter.4.cloned.1.call-start = ((), (), s32[]{:S(2)}) async-start(), calls=%async_computation.6 | async-start | bytes 4718592 | tf_op jit(solution)/shard_map/reduce_scatter | solution.py:100
  442.5 128.2 %copy-start.4 = (bf16[16,512,128]{2,1,0:T(8,128)(2,1)S(1)}, bf16[16,512,128]{2,1,0:T(8,128)(2,1)}, u32[]{:S(2)}) copy-start(bf16[16,512,128]{2,1,0:T(8,128)(2,1)} %param.19) | copy-start | bytes 6291460
  442.5 210.7 %reduce-scatter.8.cloned.1.call-start = ((), (), s32[]{:S(2)}) async-start(), calls=%async_computation.8 | async-start | bytes 2064384 | tf_op jit(solution)/shard_map/reduce_scatter | solution.py:114
  572.9 80.3 %copy-start.6 = (bf16[64,896]{1,0:T(8,128)(2,1)S(1)}, bf16[64,896]{1,0:T(8,128)(2,1)}, u32[]{:S(2)}) copy-start(bf16[64,896]{1,0:T(8,128)(2,1)} %param.24) | copy-start | bytes 344068
  586.4 124.3 %copy-start.10 = (s32[4,64]{1,0:T(4,128)S(1)}, s32[4,64]{1,0:T(4,128)}, u32[]{:S(2)}) copy-start(s32[4,64]{1,0:T(4,128)} %param.29) | copy-start | bytes 3076
  586.4 152.6 %all-gather.11.cloned.1.call-start = ((), (), s32[]{:S(2)}) async-start(), calls=%async_computation.9 | async-start | bytes 4587520 | tf_op jit(solution)/shard_map/all_gather | solution.py:129
  753.1 39.3 %copy-start.2 = (f32[256,2048]{1,0:T(8,128)}, f32[256,2048]{1,0:T(8,128)S(1)}, u32[]{:S(2)}) copy-start(f32[256,2048]{1,0:T(8,128)S(1)} %get-tuple-element.16) | copy-start | bytes 6291460
  792.8 51.4 %copy-start.1 = (bf16[16,128,512]{2,1,0:T(8,128)(2,1)S(1)}, bf16[16,128,512]{2,1,0:T(8,128)(2,1)}, u32[]{:S(2)}) copy-start(bf16[16,128,512]{2,1,0:T(8,128)(2,1)} %param.18) | copy-start | bytes 6291460
Sparse Core Ops, SparseCore 0:
  10.1 51.8 all-gather.6
  64.1 122.9 all-gather.4
  189.3 226.0 all-gather.8
  419.2 60.6 reduce-scatter.5
  483.3 87.3 reduce-scatter.3
  586.6 66.5 reduce-scatter.7
  710.7 28.3 all-gather.10
where the time goes:
time: 852 us; the launch traced here: 851 us
  waiting for transfers between devices  499 us (59%)
  blocking collectives  172 us (20%)
  matrix products  121 us (14%)
  other arithmetic  27.2 us (3%)
  local copies, waits for them, and re-layouts  15.8 us (2%)
  between operations  15.7 us (2%)
    all_gather x1, waiting for transfers between devices, body(): lax.all_gather(absorb_v, 'seq', axis=0, tiled=True)  127 us
    all_gather x1, waiting for transfers between devices, body(): lax.all_gather(query_latent, 'seq', axis=2, tiled=True)  104 us
    reduce_scatter x1, waiting for transfers between devices, body(): lax.psum_scatter(projected, 'seq', scatter_dimension=1, tiled=True)  90 us
    reduce_scatter x1, waiting for transfers between devices, body(): lax.psum_scatter(branch_term, 'seq', scatter_dimension=1, tiled=True)  65.9 us
    all_gather x1, waiting for transfers between devices, body(): lax.all_gather(q_rope, 'seq', axis=2, tiled=True)  46.8 us
    psum x1, blocking collectives, body(): lax.psum((jnp.sum(jnp.exp(logits - best[:, None]), axis=1), picked), ('se...  41 us
    pmax x1, blocking collectives, body(): best = lax.pmax(local_best, ('seq', 'batch'))  39.3 us
    pmax x1, blocking collectives, body(): row_top = lax.pmax(local_top, 'seq')  37.2 us
  transfers between devices with their start and end apart: 7, of which 7 were waited for; matrix products, arithmetic and copies ran while one was open for 14% of the time, Pallas kernels for 0%

commit v1 on v0

--- a/solution.py
+++ b/solution.py
@@ -124,12 +124,23 @@
     hidden_out = stream_mine.astype(jnp.bfloat16)
     vocab_rows = lm_head.shape[0]
     vocab_first = lax.axis_index(("seq", "batch")) * vocab_rows
-    logits = jnp.einsum(
-        "rd,vd->rv",
-        lax.all_gather(normed, "batch", axis=0, tiled=True),
-        lm_head,
-        preferred_element_type=jnp.float32,
-    )
+    u = normed
+    prior = jax.lax.axis_size("batch")
+    wide_out, carry, f_now = (prior, jax.lax.axis_index("batch"), u.shape[0])
+    pile = []
+    for nth in [*range(wide_out)]:
+        high = (
+            jax.lax.ppermute(
+                u, axis_name="batch", perm=[(t, (t + 1) % wide_out) for t in range(wide_out)]
+            )
+            if nth + 1 < wide_out
+            else u
+        )
+        a_next = jnp.einsum("rd,vd->rv", u, lm_head, preferred_element_type=jnp.float32)
+        pile.append(a_next)
+        u = high
+    d_next = jnp.concatenate(pile[::-1], axis=0)
+    logits = jnp.roll(d_next, (carry + 1) * pile[0].shape[0], axis=0)
     request_total = parent.shape[0]
     parent_rows = (
         jnp.arange(request_total, dtype=jnp.int32)[:, None] * draft_count + parent

time: 852 us -> 919 us (1.079)
  matrix products: 121 us -> 168 us
    dot_general x1 -> x4, matrix products: 14 us -> 60.3 us  [body(): jnp.einsum('rd,vd->rv', u, lm_head, preferred_element_type=jnp.float32)]
    ppermute x0 -> x3, waiting for transfers between devices: none -> 37.8 us  [body(): jax.lax.ppermute(u, axis_name='batch', perm=[(t, (t + 1) % wide_out) for...]
    all_gather x1 -> x0, waiting for transfers between devices: 27.6 us -> none  [body(): lax.all_gather(normed, 'batch', axis=0, tiled=True)]
  transfers between devices with their start and end apart: 7 -> 9, of which waited for: 7 -> 9; matrix products, arithmetic and copies ran while one was open for 14% -> 13% of each run, Pallas kernels for 0% -> 0%
where the time goes in v1:
time: 919 us; the launch traced here: 910 us
  waiting for transfers between devices  507 us (55%)
  blocking collectives  169 us (18%)
  matrix products  168 us (18%)
  other arithmetic  29.9 us (3%)
  local copies, waits for them, and re-layouts  19.2 us (2%)
  between operations  16.2 us (2%)
    all_gather x1, waiting for transfers between devices, body(): lax.all_gather(absorb_v, 'seq', axis=0, tiled=True)  126 us
    all_gather x1, waiting for transfers between devices, body(): lax.all_gather(query_latent, 'seq', axis=2, tiled=True)  104 us
    reduce_scatter x1, waiting for transfers between devices, body(): lax.psum_scatter(projected, 'seq', scatter_dimension=1, tiled=True)  90 us
    reduce_scatter x1, waiting for transfers between devices, body(): lax.psum_scatter(branch_term, 'seq', scatter_dimension=1, tiled=True)  65.9 us
    dot_general x4, matrix products, body(): jnp.einsum('rd,vd->rv', u, lm_head, preferred_element_type=jnp.float32)  60.3 us
    all_gather x1, waiting for transfers between devices, body(): lax.all_gather(q_rope, 'seq', axis=2, tiled=True)  46.8 us
    psum x1, blocking collectives, body(): lax.psum((jnp.sum(jnp.exp(logits - best[:, None]), axis=1), picked), ('se...  42.3 us
    ppermute x3, waiting for transfers between devices, body(): jax.lax.ppermute(u, axis_name='batch', perm=[(t, (t + 1) % wide_out) for...  37.8 us
  transfers between devices with their start and end apart: 9, of which 9 were waited for; matrix products, arithmetic and copies ran while one was open for 13% of the time, Pallas kernels for 0%

profile of v1, /device:TPU:0, one launch (start us, length us, event | category | flops | bytes accessed | tf_op | source)
XLA Modules:
  0.0 909.6 jit_solution(1986408705411407247)
XLA Ops:
  7.2 1.9 copy.79
  9.2 2.4 fusion.25
  11.7 0.7 all-gather.8.cloned.1.call-update
  12.4 0.2 fusion.68
  12.7 0.2 convolution_add_fusion.5
  12.9 0.2 fusion.81
  13.0 0.2 convolution_add_fusion.4
  13.2 0.2 fusion.82
  13.4 0.2 convolution_add_fusion.3
  13.5 0.2 fusion.83
  13.7 0.2 convolution_add_fusion.2
  13.9 0.2 fusion.84
  14.0 0.2 convolution_add_fusion.1
  14.2 0.2 fusion.41
  14.4 0.1 copy.82
  15.2 46.8 %all-gather.6.cloned.1.call-done = bf16[1,64,128,64]{3,1,0,2:T(8,128)(2,1)} async-done(((bf16[1,64,16,64]{3,1,0,2:T(8,128)(2,1)}), bf16[1,64,128,64]{3,1,0,2:T(8,128)(2,1)}) %all-gather.6.cloned.1.call-update) | async-done | bytes 1048592 | tf_op jit(solution)/shard_map/all_gather | solution.py:53
  62.0 3.5 copy.80
  65.5 4.1 fusion.20
  69.6 13.3 %fusion.42 = f32[1024,64,128]{0,2,1:T(8,128)} fusion(bf16[1,64,128,64]{2,3,1,0:T(8,128)(2,1)S(1)} %copy.80, bf16[1,1024,64]{1,2,0:T(8,128)(2,1)S(1)} %copy-done.7), kind=kOutput, calls=%fused_computation.42 | convolution fusion | flops 1073741824 | bytes 34734080 | tf_op jit(solution)/shard_map/rihe,rte->rhit/dot_general | solution.py:58
  82.9 104.3 %all-gather.4.cloned.1.call-done = bf16[1,64,128,512]{3,1,0,2:T(8,128)(2,1)} async-done(((bf16[1,64,16,512]{3,1,0,2:T(8,128)(2,1)}), bf16[1,64,128,512]{3,1,0,2:T(8,128)(2,1)}) %all-gather.4.cloned.1.call-update) | async-done | bytes 8388624 | tf_op jit(solution)/shard_map/all_gather | solution.py:52
  187.1 10.7 %fusion.80 = (f32[128,64]{1,0:T(8,128)S(1)}, f32[1,128,64,64]{2,3,1,0:T(8,128)}) fusion(f32[64,64,128]{1,0,2:T(8,128)} %fusion.20, bf16[1,64,512]{2,1,0:T(8,128)(2,1)S(1)} %copy-done.8, bf16[1,64,128,512]{3,1,0,2:T(8,128)(2,1)} %all-gather.4.cloned.1.call-done, pred[64,64]{0,1:T(8,128)(4,1)S(1)} %copy.82), kind=kOutput, calls=%fused_computation.103 | convolution fusion | flops 538959872 | bytes 12685312 | tf_op jit(solution)/shard_map/rihc,rjc->rhij/dot_general | solution.py:64
  197.9 32.5 %bitcast_reduce_fusion = (f32[128,64]{0,1:T(8,128)S(1)}, f32[1,1024,64,128]{1,3,2,0:T(8,128)}) fusion(f32[1024,64,128]{0,2,1:T(8,128)} %fusion.42, bf16[1,1024,512]{2,1,0:T(8,128)(2,1)S(1)} %copy-done.5, bf16[1,64,128,512]{3,1,0,2:T(8,128)(2,1)} %all-gather.4.cloned.1.call-done, pred[1024]{0:T(1024)(128)(4,1)S(1)} %add_compare_fusion), kind=kOutput, calls=%fused_computation.3 | convolution fusion | flops 8623480832 | bytes 76579840 | tf_op jit(solution)/shard_map/rihc,rtc->rhit/dot_general | solution.py:55
  230.4 37.5 %pmax.14 = f32[1,128,64]{1,2,0:T(8,128)S(1)} all-reduce(f32[1,128,64]{1,2,0:T(8,128)S(1)} %maximum_bitcast_fusion), channel_id=1, replica_groups=mesh['seq'=8,'batch'=4] {'seq'}, use_global_device_ids=true, to_apply=%region_2.3 | all-reduce | flops 8192 | bytes 65536 | tf_op jit(solution)/shard_map/pmax | solution.py:74
  268.0 20.5 %fusion.2 = (f32[128,64]{0,1:T(8,128)S(1)}, bf16[128,64,1024]{2,0,1:T(8,128)(2,1)}) fusion(f32[1,1024,64,128]{1,3,2,0:T(8,128)} %get-tuple-element.14, f32[128,64]{0,1:T(8,128)S(1)} %bitcast.166), kind=kLoop, calls=%fused_computation.8 | loop fusion | flops 25157632 | bytes 50397184 | tf_op jit(solution)/shard_map/reduce_sum | solution.py:76
  288.5 0.7 copy.89
  289.3 126.0 %all-gather.8.cloned.1.call-done = bf16[128,512,128]{2,1,0:T(8,128)(2,1)} async-done(((bf16[16,512,128]{2,1,0:T(8,128)(2,1)}), bf16[128,512,128]{2,1,0:T(8,128)(2,1)}) %all-gather.8.cloned.1.call-update) | async-done | bytes 16777232 | tf_op jit(solution)/shard_map/all_gather | solution.py:96
  415.3 27.1 %fusion.17 = f32[1,128,64,128]{3,2,1,0:T(8,128)} fusion(bf16[128,512,128]{2,1,0:T(8,128)(2,1)} %all-gather.8.cloned.1.call-done, bf16[128,64,1024]{2,0,1:T(8,128)(2,1)} %get-tuple-element.10, bf16[1,1024,512]{2,1,0:T(8,128)(2,1)S(1)} %copy-done.5), kind=kOutput, calls=%fused_computation.21 | convolution fusion | flops 9663676416 | bytes 38797312 | tf_op jit(solution)/shard_map/rhic,hcn->rhin/dot_general | solution.py:93
  442.5 0.1 constant_dynamic-slice_fusion.2
  442.6 1.3 fusion.47
  443.9 0.1 copy.100
  444.0 35.8 %reduce-scatter.6.cloned.1.call-done = f32[1,16,64]{2,0,1:T(1,128)} async-done(((f32[1,128,64]{2,0,1:T(1,128)}), f32[1,16,64]{2,0,1:T(1,128)}) %reduce-scatter.6.cloned.1.call-update) | async-done | bytes 4112 | tf_op jit(solution)/shard_map/reduce_scatter | solution.py:101
  479.7 0.8 copy.91
  480.6 90.0 %reduce-scatter.4.cloned.1.call-done = f32[1,16,64,128]{3,2,1,0:T(8,128)} async-done(((f32[1,128,64,128]{3,2,1,0:T(8,128)}), f32[1,16,64,128]{3,2,1,0:T(8,128)}) %reduce-scatter.4.cloned.1.call-update) | async-done | bytes 524304 | tf_op jit(solution)/shard_map/reduce_scatter | solution.py:100
  570.6 2.0 fusion.38
  572.6 0.2 copy.93
  572.8 13.5 %fusion.52 = f32[64,7168]{1,0:T(8,128)} fusion(bf16[2048,7168]{1,0:T(8,128)(2,1)} %param.25, bf16[8,8,16,128]{3,2,1,0:T(8,128)(2,1)S(1)} %bitcast.165), kind=kOutput, calls=%fused_computation.50 | convolution fusion | flops 1879048192 | bytes 31457280 | tf_op jit(solution)/shard_map/dot_general | solution.py:111
  586.3 0.8 dynamic_slice.22
  587.1 65.9 %reduce-scatter.8.cloned.1.call-done = f32[64,896]{1,0:T(8,128)} async-done(((f32[64,7168]{1,0:T(8,128)}), f32[64,896]{1,0:T(8,128)}) %reduce-scatter.8.cloned.1.call-update) | async-done | bytes 229392 | tf_op jit(solution)/shard_map/reduce_scatter | solution.py:114
  653.1 1.1 multiply_reduce_fusion
  654.1 19.4 %psum.21 = f32[64]{0:T(128)S(1)} all-reduce(f32[64]{0:T(128)S(1)} %multiply_reduce_fusion), channel_id=1, replica_groups=mesh['seq'=8,'batch'=4] {'seq'}, use_global_device_ids=true, to_apply=%region_9.10 | all-reduce | flops 64 | bytes 512 | tf_op jit(solution)/shard_map/psum | solution.py:117
  673.5 1.6 multiply_convert_fusion
  675.1 32.8 %all_gather.15 = bf16[64,7168]{1,0:T(8,128)(2,1)S(1)} all-gather(bf16[64,896]{1,0:T(8,128)(2,1)S(1)} %get-tuple-element.11), channel_id=1, replica_groups=mesh['seq'=8,'batch'=4] {'seq'}, dimensions={1}, use_global_device_ids=true | all-gather | bytes 1032192 | tf_op jit(solution)/shard_map/all_gather | solution.py:123
  707.9 12.8 %collective-permute-done = bf16[64,7168]{1,0:T(8,128)(2,1)S(1)} collective-permute-done((bf16[64,7168]{1,0:T(8,128)(2,1)S(1)}, bf16[64,7168]{1,0:T(8,128)(2,1)S(1)}, u32[]{:S(2)}, u32[]{:S(2)}) %collective-permute-start) | collective-permute-done | bytes 917536 | tf_op jit(solution)/shard_map/ppermute | solution.py:133
  720.7 12.9 %collective-permute-done.1 = bf16[64,7168]{1,0:T(8,128)(2,1)} collective-permute-done((bf16[64,7168]{1,0:T(8,128)(2,1)S(1)}, bf16[64,7168]{1,0:T(8,128)(2,1)}, u32[]{:S(2)}, u32[]{:S(2)}) %collective-permute-start.1) | collective-permute-done | bytes 917536 | tf_op jit(solution)/shard_map/ppermute | solution.py:133
  733.7 0.1 reshape.346
  733.8 0.1 eq.77
  734.6 12.1 %collective-permute-done.2 = bf16[64,7168]{1,0:T(8,128)(2,1)S(1)} collective-permute-done((bf16[64,7168]{1,0:T(8,128)(2,1)}, bf16[64,7168]{1,0:T(8,128)(2,1)S(1)}, u32[]{:S(2)}, u32[]{:S(2)}) %collective-permute-start.2) | collective-permute-done | bytes 917536 | tf_op jit(solution)/shard_map/ppermute | solution.py:133
  746.7 15.0 %constant_dynamic-update-slice_fusion.7 = (f32[512,2048]{1,0:T(8,128)}, f32[64,2048]{1,0:T(8,128)S(1)}) fusion(bf16[64,7168]{1,0:T(8,128)(2,1)S(1)} %collective-permute-done.2, bf16[2048,7168]{1,0:T(8,128)(2,1)} %param.27), kind=kOutput, calls=%fused_computation.79 | convolution fusion | flops 1879048192 | bytes 31326208 | tf_op jit(solution)/shard_map/rd,vd->rv/dot_general | solution.py:139
  761.7 15.2 %constant_dynamic-update-slice_fusion.6 = (f32[512,2048]{1,0:T(8,128)}, f32[64,2048]{1,0:T(8,128)S(1)}) fusion(f32[512,2048]{1,0:T(8,128)} %get-tuple-element.17, bf16[64,7168]{1,0:T(8,128)(2,1)} %collective-permute-done.1, bf16[2048,7168]{1,0:T(8,128)(2,1)} %param.27), kind=kOutput, calls=%fused_computation.78 | convolution fusion | flops 1879048192 | bytes 31326208 | tf_op jit(solution)/shard_map/rd,vd->rv/dot_general | solution.py:139
  776.9 15.0 %constant_dynamic-update-slice_fusion.5 = (f32[512,2048]{1,0:T(8,128)}, f32[64,2048]{1,0:T(8,128)S(1)}) fusion(f32[512,2048]{1,0:T(8,128)} %get-tuple-element.19, bf16[64,7168]{1,0:T(8,128)(2,1)S(1)} %collective-permute-done, bf16[2048,7168]{1,0:T(8,128)(2,1)} %param.27), kind=kOutput, calls=%fused_computation.77 | convolution fusion | flops 1879048192 | bytes 31326208 | tf_op jit(solution)/shard_map/rd,vd->rv/dot_general | solution.py:139
  791.9 15.0 %constant_dynamic-update-slice_fusion.4 = (f32[512,2048]{1,0:T(8,128)}, f32[64,2048]{1,0:T(8,128)S(1)}) fusion(f32[512,2048]{1,0:T(8,128)} %get-tuple-element.21, bf16[64,7168]{1,0:T(8,128)(2,1)S(1)} %all_gather.15, bf16[2048,7168]{1,0:T(8,128)(2,1)} %param.27), kind=kOutput, calls=%fused_computation.76 | convolution fusion | flops 1879048192 | bytes 31326208 | tf_op jit(solution)/shard_map/rd,vd->rv/dot_general | solution.py:139
  806.9 0.8 constant_dynamic-update-slice_fusion.3
  807.8 0.8 constant_dynamic-update-slice_fusion.2
  808.6 0.8 constant_dynamic-update-slice_fusion.1
  809.4 0.8 constant_dynamic-update-slice_fusion
  810.3 1.8 fusion.79
  812.1 37.1 %pmax.15 = f32[256]{0:T(256)S(1)} all-reduce(f32[256]{0:T(256)S(1)} %get-tuple-element.7), channel_id=1, replica_groups=mesh['seq'=8,'batch'=4] {'seq','batch'}, use_global_device_ids=true, to_apply=%region_13.14 | all-reduce | flops 256 | bytes 2048 | tf_op jit(solution)/shard_map/pmax | solution.py:154
  849.2 0.4 exponential_reduce_fusion
  849.7 5.3 gather_fusion
  855.0 1.9 select_reduce_fusion
  856.9 42.3 %all-reduce = (f32[256]{0:T(256)S(1)}, f32[256]{0:T(256)S(1)}) all-reduce(f32[256]{0:T(256)S(1)} %select_reduce_fusion, f32[256]{0:T(256)S(1)} %exponential_reduce_fusion), channel_id=1, replica_groups=mesh['seq'=8,'batch'=4] {'seq','batch'}, use_global_device_ids=true, to_apply=%region_11.12 | all-reduce | flops 512 | bytes 4096 | tf_op jit(solution)/shard_map/psum | solution.py:155
  899.2 1.9 gather_fusion.1
  901.2 0.1 reshape.347
  901.2 1.1 fusion.78
  (54 shorter events, 0.7 us)
Async XLA Ops:
  7.2 2.0 copy-start
  7.2 5.2 copy-start.11
  7.2 54.8 %all-gather.6.cloned.1.call-start = ((), (), s32[]{:S(2)}) async-start(), calls=%async_computation.4 | async-start | bytes 2359296 | tf_op jit(solution)/shard_map/all_gather | solution.py:53
  9.1 178.0 %all-gather.4.cloned.1.call-start = ((), (), s32[]{:S(2)}) async-start(), calls=%async_computation.3 | async-start | bytes 9437184 | tf_op jit(solution)/shard_map/all_gather | solution.py:52
  11.6 53.9 %copy-start.9 = (bf16[1,64,64]{2,1,0:T(8,128)(2,1)S(1)}, bf16[1,64,64]{2,1,0:T(8,128)(2,1)}, u32[]{:S(2)}) copy-start(bf16[1,64,64]{2,1,0:T(8,128)(2,1)} %param.23) | copy-start | bytes 24580
  11.6 403.7 %all-gather.8.cloned.1.call-start = ((), (), s32[]{:S(2)}) async-start(), calls=%async_computation.5 | async-start | bytes 18874368 | tf_op jit(solution)/shard_map/all_gather | solution.py:96
  12.3 467.4 %reduce-scatter.6.cloned.1.call-start = ((), (), s32[]{:S(2)}) async-start(), calls=%async_computation.7 | async-start | bytes 73728 | tf_op jit(solution)/shard_map/reduce_scatter | solution.py:101
  15.2 54.4 %copy-start.7 = (bf16[1,1024,64]{1,2,0:T(8,128)(2,1)S(1)}, bf16[1,1024,64]{1,2,0:T(8,128)(2,1)}, u32[]{:S(2)}) copy-start(bf16[1,1024,64]{1,2,0:T(8,128)(2,1)} %param.21) | copy-start | bytes 393220
  62.0 3.5 copy-start.3
  69.6 117.6 %copy-start.8 = (bf16[1,64,512]{2,1,0:T(8,128)(2,1)S(1)}, bf16[1,64,512]{2,1,0:T(8,128)(2,1)}, u32[]{:S(2)}) copy-start(bf16[1,64,512]{2,1,0:T(8,128)(2,1)} %param.22) | copy-start | bytes 196612
  82.9 115.0 %copy-start.5 = (bf16[1,1024,512]{2,1,0:T(8,128)(2,1)S(1)}, bf16[1,1024,512]{2,1,0:T(8,128)(2,1)}, u32[]{:S(2)}) copy-start(bf16[1,1024,512]{2,1,0:T(8,128)(2,1)} %param.20) | copy-start | bytes 3145732
  289.2 281.4 %reduce-scatter.4.cloned.1.call-start = ((), (), s32[]{:S(2)}) async-start(), calls=%async_computation.6 | async-start | bytes 4718592 | tf_op jit(solution)/shard_map/reduce_scatter | solution.py:100
  442.4 128.2 %copy-start.4 = (bf16[16,512,128]{2,1,0:T(8,128)(2,1)S(1)}, bf16[16,512,128]{2,1,0:T(8,128)(2,1)}, u32[]{:S(2)}) copy-start(bf16[16,512,128]{2,1,0:T(8,128)(2,1)} %param.19) | copy-start | bytes 6291460
  442.4 210.6 %reduce-scatter.8.cloned.1.call-start = ((), (), s32[]{:S(2)}) async-start(), calls=%async_computation.8 | async-start | bytes 2064384 | tf_op jit(solution)/shard_map/reduce_scatter | solution.py:114
  572.8 80.3 %copy-start.6 = (bf16[64,896]{1,0:T(8,128)(2,1)S(1)}, bf16[64,896]{1,0:T(8,128)(2,1)}, u32[]{:S(2)}) copy-start(bf16[64,896]{1,0:T(8,128)(2,1)} %param.24) | copy-start | bytes 344068
  572.8 161.0 %copy-start.10 = (s32[4,64]{1,0:T(4,128)S(1)}, s32[4,64]{1,0:T(4,128)}, u32[]{:S(2)}) copy-start(s32[4,64]{1,0:T(4,128)} %param.29) | copy-start | bytes 3076
  707.9 12.8 %collective-permute-start = (bf16[64,7168]{1,0:T(8,128)(2,1)S(1)}, bf16[64,7168]{1,0:T(8,128)(2,1)S(1)}, u32[]{:S(2)}, u32[]{:S(2)}) collective-permute-start(bf16[64,7168]{1,0:T(8,128)(2,1)S(1)} %all_gather.15), channel_id=1, source_target_pairs={{0,1},{1,2},{2,3},{3,0},{4,5},{5,6},{6,7},{7,4},{8,9},{9,10},{10,1... | collective-permute-start | bytes 2752520 | tf_op jit(solution)/shard_map/ppermute | solution.py:133
  720.7 12.9 %collective-permute-start.1 = (bf16[64,7168]{1,0:T(8,128)(2,1)S(1)}, bf16[64,7168]{1,0:T(8,128)(2,1)}, u32[]{:S(2)}, u32[]{:S(2)}) collective-permute-start(bf16[64,7168]{1,0:T(8,128)(2,1)S(1)} %collective-permute-done), channel_id=1, source_target_pairs={{0,1},{1,2},{2,3},{3,0},{4,5},{5,6},{6,7},{7,4},{8,9},{9,10},{10,1... | collective-permute-start | bytes 2752520 | tf_op jit(solution)/shard_map/ppermute | solution.py:133
  733.6 13.0 %collective-permute-start.2 = (bf16[64,7168]{1,0:T(8,128)(2,1)}, bf16[64,7168]{1,0:T(8,128)(2,1)S(1)}, u32[]{:S(2)}, u32[]{:S(2)}) collective-permute-start(bf16[64,7168]{1,0:T(8,128)(2,1)} %collective-permute-done.1), channel_id=1, source_target_pairs={{0,1},{1,2},{2,3},{3,0},{4,5},{5,6},{6,7},{7,4},{8,9},{9,10},{10,1... | collective-permute-start | bytes 2752520 | tf_op jit(solution)/shard_map/ppermute | solution.py:133
  812.1 37.1 %copy-start.2 = (f32[256,2048]{1,0:T(8,128)}, f32[256,2048]{1,0:T(8,128)S(1)}, u32[]{:S(2)}) copy-start(f32[256,2048]{1,0:T(8,128)S(1)} %get-tuple-element.8) | copy-start | bytes 6291460
  849.6 52.7 %copy-start.1 = (bf16[16,128,512]{2,1,0:T(8,128)(2,1)S(1)}, bf16[16,128,512]{2,1,0:T(8,128)(2,1)}, u32[]{:S(2)}) copy-start(bf16[16,128,512]{2,1,0:T(8,128)(2,1)} %param.18) | copy-start | bytes 6291460
Sparse Core Ops, SparseCore 0:
  10.1 51.8 all-gather.5
  64.1 122.9 all-gather.3
  189.3 225.9 all-gather.7
  419.1 60.5 reduce-scatter.5
  483.2 87.3 reduce-scatter.3
  586.4 66.5 reduce-scatter.7
